TPU v7x, 768 devices: a whole 4x8x12 slice. The times are simulated.
768 devices in a mesh: owner: 16 (over z_hi, x, core), shard: 48 (over y, z_lo).
Axes of the slice: x: 4, y: 8, z: 12 (z_hi: 2, z_lo: 6; z = z_hi * 6 + z_lo), core: 2. Of those that a mesh axis runs over, the one named last changes fastest.
Arguments:
- tokens: bfloat16 [576, 7168], P('shard', 'owner'), may hold values from -6 to 6
- expert_ids: int32 [576, 8], P('shard'), may hold values from 0 to 47, all different within a row; in each aligned block of 12 rows (0 to 11, 12 to 23, ...) at most 3 rows name the same one
- gate_weight: bfloat16 [48, 7168, 1024], P('shard', 'owner'), may hold values from -0.0625 to 0.0625
- up_weight: bfloat16 [48, 7168, 1024], P('shard', 'owner'), may hold values from -0.0625 to 0.0625
- trainer_down: float32 [48, 1024, 7168], P('shard', None, 'owner'), may hold values from -0.1875 to 0.1875
Outputs:
- hidden: bfloat16 [144, 48, 1024], P('owner', 'shard')
- new_down: bfloat16 [48, 1024, 7168], P('shard', 'owner')
Inputs may be any that keep to these rules, and one draw needn't show every extreme that they name: `expert_ids`: within the rows of one index of shard (aligned blocks of 12 rows) no expert is named by more than 3 rows, a bound that some block reaches.
All inputs are finite; a program needn't handle non-finite values.
Results may differ from a plain program's by a relative error of at most 0.0017.
Values may be sent and summed in bfloat16 or wider, within the bound.
No kernel may reach another device: no remote copies, remote signals or barrier semaphores. Data moves between devices by JAX's collectives and lax.ppermute only.
A program may use at most 32 MiB of HBM per device.

v0:
```python
import jax
import jax.numpy as jnp
from jax import lax
from jax.sharding import PartitionSpec as P

TOP = 8
FF = 1024
EXPERTS = 48
CAP = 3


def in_blocks(shard, dim, length):
    lengths = shard.shape
    tiles = shard.reshape(*lengths[:dim], length, lengths[dim] // length, *lengths[dim + 1 :])
    return jnp.moveaxis(tiles, dim, 0)


def sent_and_summed(shard, axis, dim):
    tiles = in_blocks(shard, dim, lax.axis_size(axis))
    arrived = lax.all_to_all(tiles, axis, split_axis=0, concat_axis=0, tiled=True)
    return arrived.sum(axis=0)


def on_device(tokens, expert_ids, gate_weight, up_weight, trainer_down):
    rows, width = tokens.shape
    flat = expert_ids.reshape(-1)
    hits = (flat[:, None] == jnp.arange(EXPERTS, dtype=jnp.int32)[None, :]).astype(jnp.int32)
    before = jnp.cumsum(hits, axis=0) - hits
    place = jnp.sum(before * hits, axis=1)
    target = place * EXPERTS + flat
    select = (target[:, None] == jnp.arange(CAP * EXPERTS, dtype=jnp.int32)[None, :]).astype(
        jnp.int32
    )
    select = jnp.sum(select.reshape(rows, TOP, CAP * EXPERTS), axis=1).astype(jnp.bfloat16)
    sent = jnp.einsum("rs,rd->sd", select, tokens, preferred_element_type=jnp.float32)
    sent = sent.astype(jnp.bfloat16).reshape(CAP, EXPERTS, width)
    received = lax.all_to_all(sent, "shard", split_axis=1, concat_axis=0, tiled=True)
    gate = jnp.einsum("sed,edf->sef", received, gate_weight, preferred_element_type=jnp.float32)
    up = jnp.einsum("sed,edf->sef", received, up_weight, preferred_element_type=jnp.float32)
    summed = sent_and_summed(jnp.concatenate([gate, up], axis=2), "owner", 0)
    gate_sum = summed[:, :, :FF]
    up_sum = summed[:, :, FF:]
    hidden = (jax.nn.silu(gate_sum) * up_sum).astype(jnp.bfloat16)
    new_down = lax.all_to_all(
        trainer_down.astype(jnp.bfloat16), "owner", split_axis=1, concat_axis=2, tiled=True
    )
    return (hidden, new_down)


def solution(mesh):
    in_specs = (
        P("shard", "owner"),
        P("shard", None),
        P("shard", "owner", None),
        P("shard", "owner", None),
        P("shard", None, "owner"),
    )
    out_specs = (P("owner", "shard", None), P("shard", "owner", None))
    return jax.shard_map(
        on_device, mesh=mesh, in_specs=in_specs, out_specs=out_specs, check_vma=False
    )
```

profile of v0, /device:TPU:88, one launch (start us, length us, event | category | flops | bytes accessed | tf_op | source)
XLA Modules:
  0.0 143.9 jit_solution(16119514443402406007)
XLA Ops:
  0.6 0.0 copy-start
  0.6 0.8 copy.24
  1.5 0.1 eq.29
  1.6 0.1 fusion.3
  1.7 0.1 reduce_window_sum.11
  1.8 0.2 select_reduce_fusion
  2.0 0.1 mul.26
  2.1 0.1 convert_reduce_fusion
  2.2 0.9 convolution_convert_fusion
  3.1 0.8 copy.26
  4.0 17.0 %all-to-all-start = ((bf16[3,48,448]{2,0,1:T(4,128)(2,1)}), bf16[3,48,448]{2,0,1:T(4,128)(2,1)S(1)}, u32[]{:S(2)}, u32[]{:S(2)}) async-start(bf16[3,48,448]{2,0,1:T(4,128)(2,1)} %copy.26), calls=%async_computation | async-start | bytes 393216 | tf_op jit(solution)/shard_map/all_to_all | solution.py:37
  21.0 2.6 %convert_element_type.24 = bf16[1,1024,448]{1,2,0:T(8,128)(2,1)} convert(f32[1,1024,448]{1,2,0:T(8,128)} %param.9) | non-fusion elementwise | flops 458752 | bytes 2752512 | tf_op jit(solution)/shard_map/convert_element_type | solution.py:45
  23.6 4.6 %copy.27 = bf16[1,1024,448]{2,0,1:T(2,128)(2,1)S(1)} copy(bf16[1,1024,448]{1,2,0:T(8,128)(2,1)} %convert_element_type.24) | data formatting | bytes 1835008 | tf_op jit(solution)/shard_map/convert_element_type | solution.py:45
  28.2 0.5 broadcast.18
  28.7 8.4 %reduce.1 = bf16[1024,448]{1,0:T(8,128)(2,1)} reduce(bf16[1024,1,448]{2,1,0:T(2,128)(2,1)S(1)} %bitcast.37, bf16[]{:T(256)} %broadcast.18), dimensions={1}, to_apply=%bitcast.32.reduce_sub_computation | reduce | bytes 1835010
  37.1 3.8 %reshape.51 = bf16[16,2,14336]{2,1,0:T(2,128)(2,1)} reshape(bf16[1024,448]{1,0:T(8,128)(2,1)} %reduce.1) | data formatting | bytes 1835008
  40.9 0.0 all-to-all-done
  40.9 11.4 %all-to-all-start.2 = ((bf16[16,2,14336]{2,1,0:T(2,128)(2,1)}), bf16[16,2,14336]{2,1,0:T(2,128)(2,1)S(1)}, u32[]{:S(2)}, u32[]{:S(2)}) async-start(bf16[16,2,14336]{2,1,0:T(2,128)(2,1)} %reshape.51), calls=%async_computation.2 | async-start | bytes 1835008 | tf_op jit(solution)/shard_map/all_to_all | solution.py:44
  52.2 0.0 copy-start.2
  52.3 0.1 reshape.47
  52.4 0.0 copy-done
  52.4 0.3 convolution_bitcast_fusion
  52.7 0.7 copy-done.2
  53.4 0.3 convolution_bitcast_fusion.1
  53.7 0.1 pad_maximum_fusion
  53.9 2.5 %reshape.50 = f32[16,9,1,2048]{3,2,1,0:T(1,128)} reshape(f32[144,1,2048]{2,0,1:T(8,128)S(1)} %pad_maximum_fusion) | data formatting | bytes 2359296 | tf_op jit(solution)/shard_map/reshape | solution.py:14
  56.3 30.2 %all-to-all-done.2 = bf16[16,2,14336]{2,1,0:T(2,128)(2,1)S(1)} async-done(((bf16[16,2,14336]{2,1,0:T(2,128)(2,1)}), bf16[16,2,14336]{2,1,0:T(2,128)(2,1)S(1)}, u32[]{:S(2)}, u32[]{:S(2)}) %all-to-all-start.2) | async-done | bytes 917536 | tf_op jit(solution)/shard_map/all_to_all | solution.py:44
  86.5 0.0 copy-start.1
  86.5 0.9 copy-done.1
  87.4 4.4 %all-to-all-start.1 = ((f32[16,9,1,2048]{3,2,1,0:T(1,128)}), f32[16,9,1,2048]{3,2,1,0:T(1,128)}, u32[]{:S(2)}, u32[]{:S(2)}) async-start(f32[16,9,1,2048]{3,2,1,0:T(1,128)} %reshape.50), calls=%async_computation.1 | async-start | bytes 2359296 | tf_op jit(solution)/shard_map/all_to_all | solution.py:20
  91.8 4.5 %reshape.52 = bf16[1024,1,448]{2,1,0:T(2,128)(2,1)S(1)} reshape(bf16[16,2,14336]{2,1,0:T(2,128)(2,1)} %copy-done.1) | data formatting | bytes 1835008
  96.3 0.3 copy.29
  96.6 0.6 copy.28
  97.2 2.1 %all_to_all.34 = bf16[1,64,7168]{2,1,0:T(8,128)(2,1)} reshape(bf16[1,64,16,448]{3,2,1,0:T(8,128)(2,1)S(1)} %copy.28) | data formatting | bytes 1835008 | tf_op jit(solution)/shard_map/all_to_all | solution.py:44
  99.3 42.0 %all-to-all-done.1 = f32[16,9,1,2048]{3,2,1,0:T(1,128)} async-done(((f32[16,9,1,2048]{3,2,1,0:T(1,128)}), f32[16,9,1,2048]{3,2,1,0:T(1,128)}, u32[]{:S(2)}, u32[]{:S(2)}) %all-to-all-start.1) | async-done | bytes 1179680 | tf_op jit(solution)/shard_map/all_to_all | solution.py:20
  141.3 2.0 %reduce_sum.31 = f32[9,2048]{1,0:T(8,128)S(1)} reduce(f32[16,9,1,2048]{3,2,1,0:T(1,128)} %all-to-all-done.1, f32[]{:T(128)} %constant.11.clone.1), dimensions={0,2}, to_apply=%region_3.4 | reduce | flops 276480 | bytes 1253380 | tf_op jit(solution)/shard_map/reduce_sum | solution.py:21
  143.3 0.6 fusion.2
  (2 shorter events, 0.0 us)
Async XLA Ops:
  0.6 51.8 %copy-start = (bf16[1,448,1024]{2,1,0:T(8,128)(2,1)S(1)}, bf16[1,448,1024]{2,1,0:T(8,128)(2,1)}, u32[]{:S(2)}) copy-start(bf16[1,448,1024]{2,1,0:T(8,128)(2,1)} %param.8) | copy-start | bytes 2752516
  4.0 36.9 %all-to-all-start = ((bf16[3,48,448]{2,0,1:T(4,128)(2,1)}), bf16[3,48,448]{2,0,1:T(4,128)(2,1)S(1)}, u32[]{:S(2)}, u32[]{:S(2)}) async-start(bf16[3,48,448]{2,0,1:T(4,128)(2,1)} %copy.26), calls=%async_computation | async-start | bytes 393216 | tf_op jit(solution)/shard_map/all_to_all | solution.py:37
  40.9 45.6 %all-to-all-start.2 = ((bf16[16,2,14336]{2,1,0:T(2,128)(2,1)}), bf16[16,2,14336]{2,1,0:T(2,128)(2,1)S(1)}, u32[]{:S(2)}, u32[]{:S(2)}) async-start(bf16[16,2,14336]{2,1,0:T(2,128)(2,1)} %reshape.51), calls=%async_computation.2 | async-start | bytes 1835008 | tf_op jit(solution)/shard_map/all_to_all | solution.py:44
  52.2 1.2 copy-start.2
  86.5 0.9 copy-start.1
  87.4 53.9 %all-to-all-start.1 = ((f32[16,9,1,2048]{3,2,1,0:T(1,128)}), f32[16,9,1,2048]{3,2,1,0:T(1,128)}, u32[]{:S(2)}, u32[]{:S(2)}) async-start(f32[16,9,1,2048]{3,2,1,0:T(1,128)} %reshape.50), calls=%async_computation.1 | async-start | bytes 2359296 | tf_op jit(solution)/shard_map/all_to_all | solution.py:20
where the time goes:
time: 145 us; the launch traced here: 144 us
  waiting for transfers between devices  72.1 us (50%)
  starting transfers between devices  32.8 us (23%)
  local copies, waits for them, and re-layouts  22.5 us (16%)
  other arithmetic  14.2 us (10%)
  matrix products  1.57 us (1%)
    all_to_all x1, waiting for transfers between devices, sent_and_summed(): lax.all_to_all(tiles, axis, split_axis=0, concat_axis=0, tiled=True)  42 us
    all_to_all x1, waiting for transfers between devices, on_device(): lax.all_to_all(trainer_down.astype(jnp.bfloat16), 'owner', split_axis=1,...  30.2 us
    all_to_all x1, starting transfers between devices, on_device(): lax.all_to_all(sent, 'shard', split_axis=1, concat_axis=0, tiled=True)  17 us
    unnamed x11, local copies, waits for them, and re-layouts  11.6 us
    all_to_all x1, starting transfers between devices, on_device(): lax.all_to_all(trainer_down.astype(jnp.bfloat16), 'owner', split_axis=1,...  11.4 us
    unnamed x1, other arithmetic  8.38 us
    convert_element_type x1, local copies, waits for them, and re-layouts, on_device(): trainer_down.astype(jnp.bfloat16)  4.59 us
    all_to_all x1, starting transfers between devices, sent_and_summed(): lax.all_to_all(tiles, axis, split_axis=0, concat_axis=0, tiled=True)  4.38 us
  transfers between devices with their start and end apart: 3, of which 2 were waited for; matrix products, arithmetic and copies ran while one was open for 20% of the time, Pallas kernels for 0%

commit v1 on v0

v1 whole, which is shorter than its diff:
```python
import jax
import jax.numpy as jnp
from jax import lax
from jax.experimental import pallas as pl
from jax.experimental.pallas import tpu as pltpu
from jax.sharding import PartitionSpec as P

FF = 1024
EXPERTS = 48
NX = 4
NY = 8
NZ = 6
LANES = 128
BF16 = jnp.bfloat16
F32 = jnp.float32

OCTET = [list(range(8)), list(range(8, 16))]
ALONG_X = [[h * 8 + x * 2 + c for x in range(NX)] for h in range(2) for c in range(2)]
SWAP_CORE = [(o, o ^ 1) for o in range(16)]
SWAP_HALF = [(o, o ^ 8) for o in range(16)]


def iota(shape, dim):
    return lax.broadcasted_iota(jnp.int32, shape, dim)


def vmem():
    return pl.BlockSpec(memory_space=pltpu.VMEM)


def smem():
    return pl.BlockSpec(memory_space=pltpu.SMEM)


def pack_kernel(ids_ref, tokens_ref, out_ref):
    n = EXPERTS * 16
    rows = tokens_ref.shape[0]
    width = tokens_ref.shape[1]
    ids = ids_ref[...]
    line = iota((n, rows), 0)
    expert = line >> 4
    hit = jnp.zeros((n, rows), jnp.bool_)
    for k in range(ids.shape[0]):
        hit = hit | (ids[k : k + 1, :] == expert)
    earlier = jnp.where(iota((rows, rows), 0) < iota((rows, rows), 1), 1.0, 0.0).astype(BF16)
    hits = jnp.where(hit, 1.0, 0.0)
    before = jnp.dot(hits.astype(BF16), earlier, preferred_element_type=F32)
    slot = ((line >> 2) & 3).astype(F32)
    taken = jnp.where(before == slot, hits, 0.0)
    total = jnp.zeros((n, LANES), F32)
    for b in range(4):
        part = tokens_ref[:, b * LANES : min((b + 1) * LANES, width)]
        if part.shape[1] < LANES:
            part = jnp.concatenate([part, jnp.zeros((rows, LANES - part.shape[1]), BF16)], axis=1)
        pick = jnp.where((line & 3) == b, taken, 0.0).astype(BF16)
        total = total + jnp.dot(pick, part, preferred_element_type=F32)
    out_ref[...] = total.astype(BF16)


def project_kernel(core_ref, got_ref, gate_ref, up_ref, keep_ref, send_ref):
    core = core_ref[0]
    n = EXPERTS * 16
    m = 144
    width = gate_ref.shape[0]
    line = iota((m, n), 0)
    other = jnp.where(line >= 72, 1, 0)
    line = line - other * 72
    last = jnp.where(line >= 64, 1, 0)
    xh = jnp.where(last == 1, line - 64, line >> 3)
    s = jnp.where(last == 1, 8, line & 7)
    owner = (xh & 1) * 8 + (xh >> 1) * 2 + (core ^ other)
    slot = owner * 9 + s
    block = (slot * 171) >> 9
    source = block * 16 + (slot - block * 3) * 4
    column = iota((m, n), 1)
    got = got_ref[...]
    parts = []
    for b in range(4):
        pick = jnp.where(column == source + b, 1.0, 0.0).astype(BF16)
        part = jnp.dot(pick, got, preferred_element_type=F32).astype(BF16)
        if (b + 1) * LANES > width:
            part = part[:, : width - b * LANES]
        parts.append(part)
    rows = jnp.concatenate(parts, axis=1)
    gate = jnp.dot(rows, gate_ref[...], preferred_element_type=F32)
    up = jnp.dot(rows, up_ref[...], preferred_element_type=F32)
    for p, out_ref in enumerate((keep_ref, send_ref)):
        for q in range(8):
            x, h = q // 2, q % 2
            for j in range(16):
                src = gate if j < 8 else up
                lane = (j % 8) * LANES
                at = p * 72 + q * 8
                out_ref[x, h * 144 + j * 8 : h * 144 + j * 8 + 8, :] = src[at : at + 8, lane : lane + LANES]
                at = p * 72 + 64 + q
                out_ref[x, h * 144 + 128 + j : h * 144 + 129 + j, :] = src[at : at + 1, lane : lane + LANES]


def hidden_kernel(a_ref, b_ref, out_ref):
    total = a_ref[...] + b_ref[...]

    def gated(v, u):
        return v / (1.0 + jnp.exp(-v)) * u

    tail = gated(total[128:136], total[136:144])
    for j in range(8):
        head = gated(total[j * 8 : j * 8 + 8], total[64 + j * 8 : 72 + j * 8])
        both = jnp.concatenate([head, jnp.broadcast_to(tail[j : j + 1], (8, LANES))], axis=0)
        out_ref[:, j * LANES : (j + 1) * LANES] = both.astype(BF16)[:9]


def split_kernel(down_ref, out_ref):
    low = iota((down_ref.shape[0], LANES), 1) < 64
    for k in range(4):
        a = down_ref[:, k * LANES : (k + 1) * LANES]
        b = down_ref[:, (k + 4) * LANES : (k + 5) * LANES]
        out_ref[2 * k] = jnp.where(low, a, pltpu.roll(b, 64, 1)).astype(BF16)
        out_ref[2 * k + 1] = jnp.where(low, pltpu.roll(a, 64, 1), b).astype(BF16)


def turn_kernel(half_ref, in_ref, keep_ref, send_ref):
    half = half_ref[0]
    shape = (LANES, LANES)
    eye = jnp.where((iota(shape, 0) ^ (half * 64)) == iota(shape, 1), 1.0, 0.0).astype(BF16)
    turned = lax.dot_general(eye, in_ref[...], (((1,), (1,)), ((), ())), preferred_element_type=F32)
    turned = turned.astype(BF16)
    keep_ref[...] = turned[:64]
    send_ref[...] = turned[64:]


def join_kernel(half_ref, keep_ref, got_ref, out_ref):
    half = half_ref[0]
    width = keep_ref.shape[1]
    out_ref[:, pl.ds(pl.multiple_of(half * width, LANES), width)] = keep_ref[...]
    out_ref[:, pl.ds(pl.multiple_of((1 - half) * width, LANES), width)] = got_ref[...]


def on_device(tokens, expert_ids, gate_weight, up_weight, trainer_down):
    rows, width = tokens.shape
    owner = lax.axis_index("owner")
    half = (owner // 8).astype(jnp.int32).reshape(1)
    core = (owner % 2).astype(jnp.int32).reshape(1)

    packed = pl.pallas_call(
        pack_kernel,
        out_shape=jax.ShapeDtypeStruct((EXPERTS * 16, LANES), BF16),
        in_specs=[vmem(), vmem()],
        out_specs=vmem(),
        name="pack",
    )(expert_ids.T, tokens)
    with jax.named_scope("dispatch"):
        got = lax.all_to_all(
            packed.reshape(EXPERTS, 16, LANES), "shard", split_axis=0, concat_axis=0, tiled=True
        )

    down = jnp.swapaxes(trainer_down, 1, 2).reshape(width, 1024)
    pieces = pl.pallas_call(
        split_kernel,
        grid=(4,),
        out_shape=jax.ShapeDtypeStruct((8, width, LANES), BF16),
        in_specs=[pl.BlockSpec((width // 4, 1024), lambda i: (i, 0))],
        out_specs=pl.BlockSpec((8, width // 4, LANES), lambda i: (0, i, 0)),
        name="split",
    )(down)
    with jax.named_scope("downx"):
        columns = lax.all_to_all(
            pieces, "owner", split_axis=0, concat_axis=0, tiled=True, axis_index_groups=OCTET
        )
    wide = 8 * width
    step = wide // 7
    down_keep, down_send = pl.pallas_call(
        turn_kernel,
        grid=(7,),
        out_shape=[jax.ShapeDtypeStruct((64, wide), BF16)] * 2,
        in_specs=[smem(), pl.BlockSpec((step, LANES), lambda i: (i, 0))],
        out_specs=[pl.BlockSpec((64, step), lambda i: (0, i))] * 2,
        name="turn",
    )(half, columns.reshape(wide, LANES))
    with jax.named_scope("downz"):
        down_got = lax.ppermute(down_send, "owner", SWAP_HALF)

    keep, send = pl.pallas_call(
        project_kernel,
        out_shape=[jax.ShapeDtypeStruct((NX, 288, LANES), F32)] * 2,
        in_specs=[smem()] + [vmem()] * 3,
        out_specs=[vmem()] * 2,
        name="project",
    )(core, got.reshape(EXPERTS * 16, LANES), gate_weight[0], up_weight[0])
    with jax.named_scope("sumc"):
        pair = keep + lax.ppermute(send, "owner", SWAP_CORE)
    with jax.named_scope("sumx"):
        summed = lax.all_to_all(
            pair, "owner", split_axis=0, concat_axis=0, tiled=True, axis_index_groups=ALONG_X
        ).sum(axis=0)
    summed = summed.reshape(2, 144, LANES)
    mine = lax.dynamic_index_in_dim(summed, half[0], 0, keepdims=False)
    theirs = lax.dynamic_index_in_dim(summed, 1 - half[0], 0, keepdims=False)
    with jax.named_scope("sumz"):
        added = lax.ppermute(theirs, "owner", SWAP_HALF)
    hidden = pl.pallas_call(
        hidden_kernel,
        out_shape=jax.ShapeDtypeStruct((9, FF), BF16),
        in_specs=[vmem()] * 2,
        out_specs=vmem(),
        name="hidden",
    )(mine, added)

    new_down = pl.pallas_call(
        join_kernel,
        out_shape=jax.ShapeDtypeStruct((64, 2 * wide), BF16),
        in_specs=[smem()] + [vmem()] * 2,
        out_specs=vmem(),
        name="join",
    )(half, down_keep, down_got)
    return hidden.reshape(9, 1, FF), new_down.reshape(1, 64, 2 * wide)


def solution(mesh):
    in_specs = (
        P("shard", "owner"),
        P("shard", None),
        P("shard", "owner", None),
        P("shard", "owner", None),
        P("shard", None, "owner"),
    )
    out_specs = (P("owner", "shard", None), P("shard", "owner", None))
    return jax.shard_map(
        on_device, mesh=mesh, in_specs=in_specs, out_specs=out_specs, check_vma=False
    )
```

time: 145 us -> 112 us (0.77)
  the two profiles are of different devices: /device:TPU:88 before, /device:TPU:66 now
where the time goes in v1:
time: 112 us; the launch traced here: 111 us
  waiting for transfers between devices  45.9 us (41%)
  starting transfers between devices  42.1 us (38%)
  Pallas kernels  18.3 us (16%)
  local copies, waits for them, and re-layouts  2.04 us (2%)
  other arithmetic  1.97 us (2%)
    ppermute x1, waiting for transfers between devices, on_device(): down_got = lax.ppermute(down_send, 'owner', SWAP_HALF)  30 us
    all_to_all x1, starting transfers between devices, on_device(): lax.all_to_all(packed.reshape(EXPERTS, 16, LANES), 'shard', split_axis=0,...  17.4 us
    all_to_all x1, waiting for transfers between devices, on_device(): lax.all_to_all(packed.reshape(EXPERTS, 16, LANES), 'shard', split_axis=0,...  10 us
    ppermute x1, starting transfers between devices, on_device(): down_got = lax.ppermute(down_send, 'owner', SWAP_HALF)  9.5 us
    pallas_call x1, Pallas kernels, on_device(): pl.pallas_call(turn_kernel, grid=(7,), out_shape=[jax.ShapeDtypeStruct((6...  5.22 us
    all_to_all x1, starting transfers between devices, on_device(): lax.all_to_all(pair, 'owner', split_axis=0, concat_axis=0, tiled=True, ax...  4.9 us
    all_to_all x1, starting transfers between devices, on_device(): lax.all_to_all(pieces, 'owner', split_axis=0, concat_axis=0, tiled=True,...  4.83 us
    pallas_call x1, Pallas kernels, on_device(): pl.pallas_call(split_kernel, grid=(4,), out_shape=jax.ShapeDtypeStruct((8...  3.71 us
  transfers between devices with their start and end apart: 6, of which 4 were waited for; matrix products, arithmetic and copies ran while one was open for 2% of the time, Pallas kernels for 13%

profile of v1, /device:TPU:66, one launch (start us, length us, event | category | flops | bytes accessed | tf_op | source)
XLA Modules:
  0.0 110.9 jit_solution(15403640358839612417)
XLA Ops:
  0.6 2.3 %pack.1 = bf16[768,128]{1,0:T(8,128)(2,1)} custom-call(s32[8,12]{1,0:T(8,128)} %bitcast.27, bf16[12,448]{1,0:T(8,128)(2,1)} %tokens_ref.1), custom_call_target="tpu_custom_call" | custom-call | tf_op jit(solution)/shard_map/pack/pallas_call | solution.py:144
  2.9 17.4 %all-to-all-start = ((bf16[48,16,128]{2,1,0:T(8,128)(2,1)}), bf16[48,16,128]{2,1,0:T(8,128)(2,1)S(1)}, u32[]{:S(2)}, u32[]{:S(2)}) async-start(bf16[48,16,128]{2,1,0:T(8,128)(2,1)} %bitcast.24), calls=%async_computation | async-start | bytes 393216 | tf_op jit(solution)/shard_map/dispatch/all_to_all | solution.py:152
  20.3 3.7 %split.1 = bf16[8,448,128]{2,1,0:T(8,128)(2,1)} custom-call(f32[448,1024]{1,0:T(8,128)} %bitcast.19), custom_call_target="tpu_custom_call" | custom-call | tf_op jit(solution)/shard_map/split/pallas_call | solution.py:157
  24.0 10.0 %all-to-all-done = bf16[48,16,128]{2,1,0:T(8,128)(2,1)S(1)} async-done(((bf16[48,16,128]{2,1,0:T(8,128)(2,1)}), bf16[48,16,128]{2,1,0:T(8,128)(2,1)S(1)}, u32[]{:S(2)}, u32[]{:S(2)}) %all-to-all-start) | async-done | bytes 196640 | tf_op jit(solution)/shard_map/dispatch/all_to_all | solution.py:152
  34.0 0.0 copy-start.1
  34.0 4.8 %all-to-all-start.2 = ((bf16[8,448,128]{2,1,0:T(8,128)(2,1)}), bf16[8,448,128]{2,1,0:T(8,128)(2,1)S(1)}, u32[]{:S(2)}, u32[]{:S(2)}) async-start(bf16[8,448,128]{2,1,0:T(8,128)(2,1)} %split.1), calls=%async_computation.2 | async-start | bytes 1835008 | tf_op jit(solution)/shard_map/downx/all_to_all | solution.py:166
  38.9 0.0 copy-done.1
  38.9 3.4 %project.1 = (f32[4,288,128]{2,1,0:T(8,128)}, f32[4,288,128]{2,1,0:T(8,128)}) custom-call(s32[1]{0:T(128)} %bitcast.core_ref, bf16[768,128]{1,0:T(8,128)(2,1)} %bitcast.23, bf16[448,1024]{1,0:T(8,128)(2,1)} %bitcast.20, bf16[448,1024]{1,0:T(8,128)(2,1)} %bitcast.21), custom_call_target="tpu_custom_call" | custom-call | tf_op jit(solution)/shard_map/project/pallas_call | solution.py:182
  42.2 2.0 %collective-permute-start = (f32[4,288,128]{2,1,0:T(8,128)}, f32[4,288,128]{2,1,0:T(8,128)S(1)}, u32[]{:S(2)}, u32[]{:S(2)}) collective-permute-start(f32[4,288,128]{2,1,0:T(8,128)} %get-tuple-element.7), channel_id=1, source_target_pairs={{0,48},{48,0},{96,144},{144,96},{192,240},{240,192},{288,336},{336... | collective-permute-start | bytes 1769480 | tf_op jit(solution)/shard_map/sumc/ppermute | solution.py:190
  44.3 2.1 %collective-permute-done = f32[4,288,128]{2,1,0:T(8,128)S(1)} collective-permute-done((f32[4,288,128]{2,1,0:T(8,128)}, f32[4,288,128]{2,1,0:T(8,128)S(1)}, u32[]{:S(2)}, u32[]{:S(2)}) %collective-permute-start) | collective-permute-done | bytes 589856 | tf_op jit(solution)/shard_map/sumc/ppermute | solution.py:190
  46.3 1.9 %add.17 = f32[4,288,128]{2,1,0:T(8,128)} add(f32[4,288,128]{2,1,0:T(8,128)} %get-tuple-element.6, f32[4,288,128]{2,1,0:T(8,128)S(1)} %collective-permute-done) | non-fusion elementwise | flops 147456 | bytes 1769472 | tf_op jit(solution)/shard_map/sumc/add | solution.py:190
  48.3 3.7 %all-to-all-done.2 = bf16[8,448,128]{2,1,0:T(8,128)(2,1)S(1)} async-done(((bf16[8,448,128]{2,1,0:T(8,128)(2,1)}), bf16[8,448,128]{2,1,0:T(8,128)(2,1)S(1)}, u32[]{:S(2)}, u32[]{:S(2)}) %all-to-all-start.2) | async-done | bytes 917536 | tf_op jit(solution)/shard_map/downx/all_to_all | solution.py:166
  51.9 0.0 copy-start
  51.9 4.9 %all-to-all-start.1 = ((f32[4,288,128]{2,1,0:T(8,128)}), f32[4,288,128]{2,1,0:T(8,128)S(1)}, u32[]{:S(2)}, u32[]{:S(2)}) async-start(f32[4,288,128]{2,1,0:T(8,128)} %add.17), calls=%async_computation.1 | async-start | bytes 1179648 | tf_op jit(solution)/shard_map/sumx/all_to_all | solution.py:192
  56.9 0.0 copy-done
  56.9 5.2 %turn.1 = (bf16[64,3584]{1,0:T(8,128)(2,1)}, bf16[64,3584]{1,0:T(8,128)(2,1)}) custom-call(s32[1]{0:T(128)} %bitcast.10.half_ref, bf16[3584,128]{1,0:T(8,128)(2,1)} %bitcast.18), custom_call_target="tpu_custom_call" | custom-call | tf_op jit(solution)/shard_map/turn/pallas_call | solution.py:171
  62.1 9.5 %collective-permute-start.2 = (bf16[64,3584]{1,0:T(8,128)(2,1)}, bf16[64,3584]{1,0:T(8,128)(2,1)S(1)}, u32[]{:S(2)}, u32[]{:S(2)}) collective-permute-start(bf16[64,3584]{1,0:T(8,128)(2,1)} %get-tuple-element.9), channel_id=1, source_target_pairs={{0,384},{48,432},{96,480},{144,528},{192,576},{240,624},{288,672},... | collective-permute-start | bytes 1376264 | tf_op jit(solution)/shard_map/downz/ppermute | solution.py:180
  71.6 0.0 all-to-all-done.1
  71.7 0.6 dynamic-slice_bitcast_fusion
  72.3 3.4 %collective-permute-start.1 = (f32[144,128]{1,0:T(8,128)S(1)}, f32[144,128]{1,0:T(8,128)S(1)}, u32[]{:S(2)}, u32[]{:S(2)}) collective-permute-start(f32[144,128]{1,0:T(8,128)S(1)} %get-tuple-element.10), channel_id=1, source_target_pairs={{0,384},{48,432},{96,480},{144,528},{192,576},{240,624},{288,672},... | collective-permute-start | bytes 221192 | tf_op jit(solution)/shard_map/sumz/ppermute | solution.py:199
  75.8 30.0 %collective-permute-done.2.got_ref = bf16[64,3584]{1,0:T(8,128)(2,1)S(1)} collective-permute-done((bf16[64,3584]{1,0:T(8,128)(2,1)}, bf16[64,3584]{1,0:T(8,128)(2,1)S(1)}, u32[]{:S(2)}, u32[]{:S(2)}) %collective-permute-start.2) | collective-permute-done | bytes 458784 | tf_op jit(solution)/shard_map/downz/ppermute | solution.py:180
  105.8 0.0 copy-start.2
  105.8 0.8 copy-done.2
  106.6 2.1 %join.1 = bf16[64,7168]{1,0:T(8,128)(2,1)} custom-call(s32[1]{0:T(128)} %bitcast.10.half_ref, bf16[64,3584]{1,0:T(8,128)(2,1)} %get-tuple-element.8.keep_ref, bf16[64,3584]{1,0:T(8,128)(2,1)} %copy-done.2), custom_call_target="tpu_custom_call" | custom-call | tf_op jit(solution)/shard_map/join/pallas_call | solution.py:208
  108.7 0.0 collective-permute-done.1.b_ref
  108.7 0.0 copy-start.3
  108.7 0.6 copy-done.3
  109.3 1.6 %hidden.1 = bf16[9,1024]{1,0:T(8,128)(2,1)} custom-call(f32[144,128]{1,0:T(8,128)} %get-tuple-element.11.a_ref, f32[144,128]{1,0:T(8,128)} %copy-done.3), custom_call_target="tpu_custom_call" | custom-call | tf_op jit(solution)/shard_map/hidden/pallas_call | solution.py:200
  (1 shorter events, 0.0 us)
Async XLA Ops:
  2.9 31.1 %all-to-all-start = ((bf16[48,16,128]{2,1,0:T(8,128)(2,1)}), bf16[48,16,128]{2,1,0:T(8,128)(2,1)S(1)}, u32[]{:S(2)}, u32[]{:S(2)}) async-start(bf16[48,16,128]{2,1,0:T(8,128)(2,1)} %bitcast.24), calls=%async_computation | async-start | bytes 393216 | tf_op jit(solution)/shard_map/dispatch/all_to_all | solution.py:152
  34.0 4.8 %copy-start.1 = (bf16[48,16,128]{2,1,0:T(8,128)(2,1)}, bf16[48,16,128]{2,1,0:T(8,128)(2,1)S(1)}, u32[]{:S(2)}) copy-start(bf16[48,16,128]{2,1,0:T(8,128)(2,1)S(1)} %all-to-all-done) | copy-start | bytes 589828
  34.0 17.9 %all-to-all-start.2 = ((bf16[8,448,128]{2,1,0:T(8,128)(2,1)}), bf16[8,448,128]{2,1,0:T(8,128)(2,1)S(1)}, u32[]{:S(2)}, u32[]{:S(2)}) async-start(bf16[8,448,128]{2,1,0:T(8,128)(2,1)} %split.1), calls=%async_computation.2 | async-start | bytes 1835008 | tf_op jit(solution)/shard_map/downx/all_to_all | solution.py:166
  42.2 4.1 %collective-permute-start = (f32[4,288,128]{2,1,0:T(8,128)}, f32[4,288,128]{2,1,0:T(8,128)S(1)}, u32[]{:S(2)}, u32[]{:S(2)}) collective-permute-start(f32[4,288,128]{2,1,0:T(8,128)} %get-tuple-element.7), channel_id=1, source_target_pairs={{0,48},{48,0},{96,144},{144,96},{192,240},{240,192},{288,336},{336... | collective-permute-start | bytes 1769480 | tf_op jit(solution)/shard_map/sumc/ppermute | solution.py:190
  51.9 4.9 %copy-start = (bf16[8,448,128]{2,1,0:T(8,128)(2,1)}, bf16[8,448,128]{2,1,0:T(8,128)(2,1)S(1)}, u32[]{:S(2)}) copy-start(bf16[8,448,128]{2,1,0:T(8,128)(2,1)S(1)} %all-to-all-done.2) | copy-start | bytes 2752516
  51.9 19.7 %all-to-all-start.1 = ((f32[4,288,128]{2,1,0:T(8,128)}), f32[4,288,128]{2,1,0:T(8,128)S(1)}, u32[]{:S(2)}, u32[]{:S(2)}) async-start(f32[4,288,128]{2,1,0:T(8,128)} %add.17), calls=%async_computation.1 | async-start | bytes 1179648 | tf_op jit(solution)/shard_map/sumx/all_to_all | solution.py:192
  62.1 43.7 %collective-permute-start.2 = (bf16[64,3584]{1,0:T(8,128)(2,1)}, bf16[64,3584]{1,0:T(8,128)(2,1)S(1)}, u32[]{:S(2)}, u32[]{:S(2)}) collective-permute-start(bf16[64,3584]{1,0:T(8,128)(2,1)} %get-tuple-element.9), channel_id=1, source_target_pairs={{0,384},{48,432},{96,480},{144,528},{192,576},{240,624},{288,672},... | collective-permute-start | bytes 1376264 | tf_op jit(solution)/shard_map/downz/ppermute | solution.py:180
  72.3 36.4 %collective-permute-start.1 = (f32[144,128]{1,0:T(8,128)S(1)}, f32[144,128]{1,0:T(8,128)S(1)}, u32[]{:S(2)}, u32[]{:S(2)}) collective-permute-start(f32[144,128]{1,0:T(8,128)S(1)} %get-tuple-element.10), channel_id=1, source_target_pairs={{0,384},{48,432},{96,480},{144,528},{192,576},{240,624},{288,672},... | collective-permute-start | bytes 221192 | tf_op jit(solution)/shard_map/sumz/ppermute | solution.py:199
  105.8 0.8 copy-start.2
  108.7 0.6 copy-start.3

commit v2 on v1

v2 whole, which is shorter than its diff:
```python
import jax
import jax.numpy as jnp
from jax import lax
from jax.experimental import pallas as pl
from jax.experimental.pallas import tpu as pltpu
from jax.sharding import PartitionSpec as P


FF = 1024
EXPERTS = 48
NX = 4
LANES = 128
BF16 = jnp.bfloat16
F32 = jnp.float32

OCTET = [list(range(8)), list(range(8, 16))]
ALONG_X = [[(o, o & 9 | (o + 2 * d) & 6) for o in range(16)] for d in range(NX)]
SWAP_CORE = [(o, o ^ 1) for o in range(16)]
SWAP_HALF = [(o, o ^ 8) for o in range(16)]


def iota(shape, dim):
    return lax.broadcasted_iota(jnp.int32, shape, dim)


def vmem():
    return pl.BlockSpec(memory_space=pltpu.VMEM)


def smem():
    return pl.BlockSpec(memory_space=pltpu.SMEM)


def packed(ids_ref, tokens_ref):
    n = EXPERTS * 16
    rows = tokens_ref.shape[0]
    width = tokens_ref.shape[1]
    ids = ids_ref[...]
    line = iota((n, rows), 0)
    expert = line >> 4
    hit = jnp.zeros((n, rows), jnp.bool_)
    for k in range(ids.shape[0]):
        hit = hit | (ids[k : k + 1, :] == expert)
    earlier = jnp.where(iota((rows, rows), 0) < iota((rows, rows), 1), 1.0, 0.0).astype(BF16)
    hits = jnp.where(hit, 1.0, 0.0)
    before = jnp.dot(hits.astype(BF16), earlier, preferred_element_type=F32)
    slot = ((line >> 2) & 3).astype(F32)
    taken = jnp.where(before == slot, hits, 0.0)
    total = jnp.zeros((n, LANES), F32)
    for b in range(4):
        part = tokens_ref[:, b * LANES : min((b + 1) * LANES, width)]
        if part.shape[1] < LANES:
            part = jnp.concatenate([part, jnp.zeros((rows, LANES - part.shape[1]), BF16)], axis=1)
        pick = jnp.where((line & 3) == b, taken, 0.0).astype(BF16)
        total = total + jnp.dot(pick, part, preferred_element_type=F32)
    return total.astype(BF16)


def project_kernel(core_ref, got_ref, gate_ref, up_ref, keep_ref, send_ref):
    core = core_ref[0]
    n = EXPERTS * 16
    m = 144
    width = gate_ref.shape[0]
    line = iota((m, n), 0)
    other = jnp.where(line >= 72, 1, 0)
    line = line - other * 72
    last = jnp.where(line >= 64, 1, 0)
    xh = jnp.where(last == 1, line - 64, line >> 3)
    s = jnp.where(last == 1, 8, line & 7)
    owner = (xh & 1) * 8 + (xh >> 1) * 2 + (core ^ other)
    slot = owner * 9 + s
    block = (slot * 171) >> 9
    source = block * 16 + (slot - block * 3) * 4
    column = iota((m, n), 1)
    got = got_ref[...]
    parts = []
    for b in range(4):
        pick = jnp.where(column == source + b, 1.0, 0.0).astype(BF16)
        part = jnp.dot(pick, got, preferred_element_type=F32).astype(BF16)
        if (b + 1) * LANES > width:
            part = part[:, : width - b * LANES]
        parts.append(part)
    rows = jnp.concatenate(parts, axis=1)
    gate = jnp.dot(rows, gate_ref[...], preferred_element_type=F32)
    up = jnp.dot(rows, up_ref[...], preferred_element_type=F32)
    for p, out_ref in enumerate((keep_ref, send_ref)):
        for q in range(8):
            x, h = q // 2, q % 2
            for j in range(16):
                src = gate if j < 8 else up
                lane = (j % 8) * LANES
                at = p * 72 + q * 8
                out_ref[x, h * 144 + j * 8 : h * 144 + j * 8 + 8, :] = src[at : at + 8, lane : lane + LANES]
                at = p * 72 + 64 + q
                out_ref[x, h * 144 + 128 + j : h * 144 + 129 + j, :] = src[at : at + 1, lane : lane + LANES]


def hidden_kernel(a_ref, b_ref, out_ref):
    total = a_ref[...] + b_ref[...]

    def gated(v, u):
        return v / (1.0 + jnp.exp(-v)) * u

    tail = gated(total[128:136], total[136:144])
    for j in range(8):
        head = gated(total[j * 8 : j * 8 + 8], total[64 + j * 8 : 72 + j * 8])
        both = jnp.concatenate([head, jnp.broadcast_to(tail[j : j + 1], (8, LANES))], axis=0)
        out_ref[:, j * LANES : (j + 1) * LANES] = both.astype(BF16)[:9]


def add_kernel(x_ref, a_ref, b_ref, *out_refs):
    for d, out_ref in enumerate(out_refs):
        at = (x_ref[0] + d) & 3
        out_ref[...] = a_ref[at] + b_ref[at]


def fold_kernel(half_ref, a_ref, b_ref, c_ref, d_ref, mine_ref, theirs_ref):
    half = half_ref[0]
    for at, out_ref in ((half, mine_ref), (1 - half, theirs_ref)):
        rows = pl.ds(pl.multiple_of(at * 144, 8), 144)
        out_ref[...] = (a_ref[rows] + b_ref[rows]) + (c_ref[rows] + d_ref[rows])


def quarters(parts):
    n = parts[0][0].shape[0]
    group = iota((n, LANES), 1) >> 5
    out = None
    for q, (tile, offset) in enumerate(parts):
        tile = tile.astype(F32)
        if offset != 32 * q:
            tile = pltpu.roll(tile, (32 * q - offset) % LANES, 1)
        out = tile if out is None else jnp.where(group == q, tile, out)
    return out.astype(BF16)


def prepare_kernel(half_ref, ids_ref, tokens_ref, down_ref, rows_ref, p_ref, down, rows, p, sems):
    lanes = pl.ds(pl.multiple_of((1 - half_ref[0]) * 512, LANES), 512)
    load = pltpu.make_async_copy(down_ref.at[:, lanes], down, sems.at[0])
    store_rows = pltpu.make_async_copy(rows, rows_ref, sems.at[1])
    store_p = pltpu.make_async_copy(p, p_ref, sems.at[2])
    load.start()
    rows[...] = packed(ids_ref, tokens_ref)
    store_rows.start()
    load.wait()
    for t in range(2):
        parts = []
        for j in range(4 * t, 4 * t + 4):
            k = j // 2 * LANES
            parts.append((down[:, k : k + LANES], j % 2 * 64))
        p[:, t * LANES : (t + 1) * LANES] = quarters(parts)
    store_p.start()
    store_rows.wait()
    store_p.wait()


def split_p_kernel(half_ref, down_ref, got_ref, out_ref):
    n = out_ref.shape[1]
    for j in range(8):
        k, g = j // 2 * LANES, j // 4 * LANES
        parts = []
        for w in range(2):
            rows = slice(w * n, (w + 1) * n)
            parts.append((down_ref[rows, k : k + LANES], j % 2 * 64))
            parts.append((got_ref[rows, g : g + LANES], j % 4 * 32))
        out_ref[j] = quarters(parts)


def split_q_kernel(down_ref, out_ref):
    n = out_ref.shape[1]
    for j in range(8):
        k = j // 2 * LANES
        parts = []
        for w in range(2):
            for h in range(2):
                at = h * 512 + k
                parts.append((down_ref[w * n : (w + 1) * n, at : at + LANES], j % 2 * 64 + 32))
        out_ref[j] = quarters(parts)


def load_kernel(gate_ref, up_ref, gate_out_ref, up_out_ref, sems):
    copies = [
        pltpu.make_async_copy(gate_ref, gate_out_ref, sems.at[0]),
        pltpu.make_async_copy(up_ref, up_out_ref, sems.at[1]),
    ]
    for copy in copies:
        copy.start()
    for copy in copies:
        copy.wait()


def turned(ref):
    n = ref.shape[1]
    low = iota((n, LANES), 1) < 64
    zero = jnp.zeros((n, LANES), BF16)
    parts = []
    for q in range(8):
        block = ref[q]
        parts += [jnp.where(low, block, zero), jnp.where(low, zero, block)]
    stack = jnp.concatenate(parts, axis=0)
    i, k = iota((64, LANES), 0), iota((64, LANES), 1)
    eye = jnp.where((i == k) | (i + 64 == k), 1.0, 0.0).astype(BF16)
    out = lax.dot_general(eye, stack, (((1,), (1,)), ((), ())), preferred_element_type=F32)
    return out.astype(BF16)


def turn_q_kernel(half_ref, in_ref, keep_ref, send_ref):
    rows = turned(in_ref)
    first = half_ref[0] == 0
    keep_ref[...] = jnp.where(first, rows[:32], rows[32:])
    send_ref[...] = jnp.where(first, rows[32:], rows[:32])


def join_kernel(half_ref, p_ref, keep_ref, got_ref, out_ref):
    width = keep_ref.shape[1]
    own = pl.ds(pl.multiple_of(half_ref[0] * width, LANES), width)
    other = pl.ds(pl.multiple_of((1 - half_ref[0]) * width, LANES), width)
    rows = turned(p_ref)
    out_ref[:32, own] = rows[:32]
    out_ref[:32, other] = rows[32:]
    out_ref[32:, own] = keep_ref[...]
    out_ref[32:, other] = got_ref[...]


def chip(x):
    return pltpu.with_memory_space_constraint(x, pltpu.VMEM)


def half_of_down(kernel, out, half, down, other, *more):
    width = down.shape[0]
    return pl.pallas_call(
        kernel,
        out_shape=jax.ShapeDtypeStruct(out, BF16),
        grid_spec=pltpu.PrefetchScalarGridSpec(
            num_scalar_prefetch=1,
            grid=(1,),
            in_specs=[pl.BlockSpec((width, 512), lambda i, h: (0, (1 - h[0]) if other else h[0]))]
            + [vmem() for _ in more],
            out_specs=vmem(),
        ),
    )(half, down, *more)


def over_x(x):
    return lax.all_to_all(
        x, "owner", split_axis=0, concat_axis=0, tiled=True, axis_index_groups=OCTET
    )


def on_device(tokens, expert_ids, gate_weight, up_weight, trainer_down):
    _, width = tokens.shape
    owner = lax.axis_index("owner")
    half = (owner >> 3).astype(jnp.int32).reshape(1)
    core = (owner & 1).astype(jnp.int32).reshape(1)
    place = ((owner >> 1) & 3).astype(jnp.int32).reshape(1)
    down = jnp.swapaxes(trainer_down, 1, 2).reshape(width, 1024)

    shapes = [(EXPERTS * 16, LANES), (width, 256)]
    anywhere = pl.BlockSpec(memory_space=pl.ANY)
    slots, outgoing = pl.pallas_call(
        prepare_kernel,
        out_shape=[jax.ShapeDtypeStruct(shape, BF16) for shape in shapes],
        in_specs=[smem()] + [vmem()] * 2 + [anywhere],
        out_specs=[anywhere] * 2,
        scratch_shapes=[pltpu.VMEM((width, 512), F32)]
        + [pltpu.VMEM(shape, BF16) for shape in shapes]
        + [pltpu.SemaphoreType.DMA((3,))],
        name="prepare",
    )(half, expert_ids.T, tokens, down)
    incoming = lax.ppermute(outgoing, "owner", SWAP_HALF)
    got = lax.all_to_all(
        slots.reshape(EXPERTS, 16, LANES), "shard", split_axis=0, concat_axis=0, tiled=True
    )

    pieces = (8, width // 2, LANES)
    q = pl.pallas_call(
        split_q_kernel,
        out_shape=jax.ShapeDtypeStruct(pieces, BF16),
        in_specs=[vmem()],
        out_specs=vmem(),
        name="splitq",
    )(down)
    q = over_x(q)
    q_keep, q_send = pl.pallas_call(
        turn_q_kernel,
        out_shape=[pltpu.VMEM((32, 8 * width), BF16)] * 2,
        in_specs=[smem(), vmem()],
        out_specs=[vmem()] * 2,
        name="turnq",
    )(half, chip(q))
    q_got = lax.ppermute(q_send, "owner", SWAP_HALF)

    weights = pl.pallas_call(
        load_kernel,
        out_shape=[pltpu.VMEM(gate_weight.shape[1:], BF16)] * 2,
        in_specs=[pl.BlockSpec(memory_space=pl.ANY)] * 2,
        out_specs=[vmem()] * 2,
        scratch_shapes=[pltpu.SemaphoreType.DMA((2,))],
        name="load",
    )(gate_weight[0], up_weight[0])
    keep, send = pl.pallas_call(
        project_kernel,
        out_shape=[jax.ShapeDtypeStruct((NX, 288, LANES), F32), pltpu.VMEM((NX, 288, LANES), F32)],
        in_specs=[smem()] + [vmem()] * 3,
        out_specs=[vmem()] * 2,
        name="project",
    )(core, chip(got.reshape(EXPERTS * 16, LANES)), chip(weights[0]), chip(weights[1]))
    pair = lax.ppermute(send, "owner", SWAP_CORE)
    sums = pl.pallas_call(
        add_kernel,
        out_shape=[pltpu.VMEM(keep.shape[1:], F32)] * NX,
        in_specs=[smem()] + [vmem()] * 2,
        out_specs=[vmem()] * NX,
        name="addcores",
    )(place, keep, chip(pair))
    summed = [sums[0]]
    for d in range(1, NX):
        summed.append(lax.ppermute(sums[d], "owner", ALONG_X[d]))
    mine, theirs = pl.pallas_call(
        fold_kernel,
        out_shape=[pltpu.VMEM((144, LANES), F32)] * 2,
        in_specs=[smem()] + [vmem()] * NX,
        out_specs=[vmem()] * 2,
        name="fold",
    )(half, *[chip(x) for x in summed])

    p = half_of_down(split_p_kernel, pieces, half, down, False, chip(incoming))
    p = over_x(p)

    added = lax.ppermute(theirs, "owner", SWAP_HALF)
    hidden = pl.pallas_call(
        hidden_kernel,
        out_shape=jax.ShapeDtypeStruct((9, FF), BF16),
        in_specs=[vmem()] * 2,
        out_specs=vmem(),
        name="hidden",
    )(chip(mine), chip(added))

    new_down = pl.pallas_call(
        join_kernel,
        out_shape=jax.ShapeDtypeStruct((64, 16 * width), BF16),
        in_specs=[smem()] + [vmem()] * 3,
        out_specs=vmem(),
        name="join",
    )(half, chip(p), chip(q_keep), chip(q_got))
    return hidden.reshape(9, 1, FF), new_down.reshape(1, 64, 16 * width)


def solution(mesh):
    in_specs = (
        P("shard", "owner"),
        P("shard", None),
        P("shard", "owner", None),
        P("shard", "owner", None),
        P("shard", None, "owner"),
    )
    out_specs = (P("owner", "shard", None), P("shard", "owner", None))
    return jax.shard_map(
        on_device, mesh=mesh, in_specs=in_specs, out_specs=out_specs, check_vma=False
    )
```

time: 112 us -> 120 us (1.071)
  starting transfers between devices: 42.1 us -> 61.2 us
  waiting for transfers between devices: 45.9 us -> 41.7 us
  Pallas kernels: 18.3 us -> 15.4 us
  local copies, waits for them, and re-layouts: 2.04 us -> 0.01 us
  other arithmetic: 1.97 us -> 0 us
    ppermute x2 -> x6, starting transfers between devices: 11.5 us -> 31.4 us  [the longest x3 10.4 us: on_device(): summed.append(lax.ppermute(sums[d], 'owner', ALONG_X[d]))]
    ppermute x2 -> x6, waiting for transfers between devices: 32.1 us -> 21 us  [the longest x1 16.2 us: on_device(): incoming = lax.ppermute(outgoing, 'owner', SWAP_HALF)]
    ppermute x1, waiting for transfers between devices: 0.01 us -> 8.43 us  [on_device(): added = lax.ppermute(theirs, 'owner', SWAP_HALF)]
    add x1 -> x0, other arithmetic: 1.93 us -> none  [on_device(): pair = keep + lax.ppermute(send, 'owner', SWAP_CORE)]
    pallas_call x1, Pallas kernels: 3.37 us -> 1.61 us  [on_device(): pl.pallas_call(project_kernel, out_shape=[jax.ShapeDtypeStruct((NX, 288,...]
    all_to_all x3, waiting for transfers between devices: 13.7 us -> 12.3 us  [the longest x1 12.3 us: on_device(): lax.all_to_all(slots.reshape(EXPERTS, 16, LANES), 'shard', split_axis=0,...]
    unnamed x8 -> x2, local copies, waits for them, and re-layouts: 1.39 us -> 0.01 us
    pallas_call x4 -> x8, Pallas kernels: 13.3 us -> 13.1 us  [the longest x1 2.88 us: on_device(): pl.pallas_call(prepare_kernel, out_shape=[jax.ShapeDtypeStruct(shape, BF1...]
  transfers between devices with their start and end apart: 6 -> 10, of which waited for: 4 -> 5; matrix products, arithmetic and copies ran while one was open for 2% -> 0% of each run, Pallas kernels for 13% -> 9%
where the time goes in v2:
time: 120 us; the launch traced here: 119 us
  starting transfers between devices  61.2 us (51%)
  waiting for transfers between devices  41.7 us (35%)
  Pallas kernels  15.4 us (13%)
    all_to_all x1, starting transfers between devices, on_device(): lax.all_to_all(slots.reshape(EXPERTS, 16, LANES), 'shard', split_axis=0,...  17.4 us
    ppermute x1, waiting for transfers between devices, on_device(): incoming = lax.ppermute(outgoing, 'owner', SWAP_HALF)  16.2 us
    all_to_all x1, waiting for transfers between devices, on_device(): lax.all_to_all(slots.reshape(EXPERTS, 16, LANES), 'shard', split_axis=0,...  12.3 us
    ppermute x3, starting transfers between devices, on_device(): summed.append(lax.ppermute(sums[d], 'owner', ALONG_X[d]))  10.4 us
    all_to_all x2, starting transfers between devices, over_x(): lax.all_to_all(x, 'owner', split_axis=0, concat_axis=0, tiled=True, axis_...  9.72 us
    ppermute x1, starting transfers between devices, on_device(): incoming = lax.ppermute(outgoing, 'owner', SWAP_HALF)  9.52 us
    ppermute x1, starting transfers between devices, on_device(): q_got = lax.ppermute(q_send, 'owner', SWAP_HALF)  9.47 us
    ppermute x1, waiting for transfers between devices, on_device(): added = lax.ppermute(theirs, 'owner', SWAP_HALF)  8.43 us
  transfers between devices with their start and end apart: 10, of which 5 were waited for; matrix products, arithmetic and copies ran while one was open for 0% of the time, Pallas kernels for 9%

profile of v2, /device:TPU:66, one launch (start us, length us, event | category | flops | bytes accessed | tf_op | source)
XLA Modules:
  0.0 119.1 jit_solution(10956363793959569126)
XLA Ops:
  0.6 2.9 %prepare.1 = (bf16[768,128]{1,0:T(8,128)(2,1)}, bf16[448,256]{1,0:T(8,128)(2,1)}) custom-call(s32[1]{0:T(128)} %bitcast.half_ref, s32[8,12]{1,0:T(8,128)} %bitcast.22, bf16[12,448]{1,0:T(8,128)(2,1)} %tokens_ref.1, f32[448,1024]{1,0:T(8,128)} %bitcast.14), custom_call_target="tpu_custom_call" | custom-call | tf_op jit(solution)/shard_map/prepare/pallas_call | solution.py:259
  3.5 17.4 %all-to-all-start = ((bf16[48,16,128]{2,1,0:T(8,128)(2,1)}), bf16[48,16,128]{2,1,0:T(8,128)(2,1)S(1)}, u32[]{:S(2)}, u32[]{:S(2)}) async-start(bf16[48,16,128]{2,1,0:T(8,128)(2,1)} %bitcast.20), calls=%async_computation | async-start | bytes 393216 | tf_op jit(solution)/shard_map/all_to_all | solution.py:270
  20.9 1.5 %load.1 = (bf16[448,1024]{1,0:T(8,128)(2,1)S(1)}, bf16[448,1024]{1,0:T(8,128)(2,1)S(1)}) custom-call(bf16[448,1024]{1,0:T(8,128)(2,1)} %bitcast.17, bf16[448,1024]{1,0:T(8,128)(2,1)} %bitcast.18), custom_call_target="tpu_custom_call" | custom-call | tf_op jit(solution)/shard_map/load/pallas_call | solution.py:292
  22.4 12.3 %all-to-all-done = bf16[48,16,128]{2,1,0:T(8,128)(2,1)S(1)} async-done(((bf16[48,16,128]{2,1,0:T(8,128)(2,1)}), bf16[48,16,128]{2,1,0:T(8,128)(2,1)S(1)}, u32[]{:S(2)}, u32[]{:S(2)}) %all-to-all-start) | async-done | bytes 196640 | tf_op jit(solution)/shard_map/all_to_all | solution.py:270
  34.7 1.6 %project.1 = (f32[4,288,128]{2,1,0:T(8,128)}, f32[4,288,128]{2,1,0:T(8,128)S(1)}) custom-call(s32[1]{0:T(128)} %bitcast.2.core_ref, bf16[768,128]{1,0:T(8,128)(2,1)S(1)} %bitcast.13, bf16[448,1024]{1,0:T(8,128)(2,1)S(1)} %get-tuple-element.17.gate_ref, bf16[448,1024]{1,0:T(8,128)(2,1)S(1)} %get-tuple-element.18.up_ref), custom_call_target="tpu_custom_call" | custom-call | tf_op jit(solution)/shard_map/project/pallas_call | solution.py:300
  36.3 0.0 copy-start
  36.3 2.0 %collective-permute-start = (f32[4,288,128]{2,1,0:T(8,128)S(1)}, f32[4,288,128]{2,1,0:T(8,128)S(1)}, u32[]{:S(2)}, u32[]{:S(2)}) collective-permute-start(f32[4,288,128]{2,1,0:T(8,128)S(1)} %get-tuple-element.20), channel_id=1, source_target_pairs={{0,48},{48,0},{96,144},{144,96},{192,240},{240,192},{288,336},{336... | collective-permute-start | bytes 1769480 | tf_op jit(solution)/shard_map/ppermute | solution.py:307
  38.3 2.7 %splitq.1 = bf16[8,224,128]{2,1,0:T(8,128)(2,1)} custom-call(f32[448,1024]{1,0:T(8,128)} %bitcast.15), custom_call_target="tpu_custom_call" | custom-call | tf_op jit(solution)/shard_map/splitq/pallas_call | solution.py:275
  41.0 4.9 %all-to-all-start.2 = ((bf16[8,224,128]{2,1,0:T(8,128)(2,1)}), bf16[8,224,128]{2,1,0:T(8,128)(2,1)S(1)}, u32[]{:S(2)}, u32[]{:S(2)}) async-start(bf16[8,224,128]{2,1,0:T(8,128)(2,1)} %splitq.1), calls=%async_computation.2 | async-start | bytes 917504 | tf_op jit(solution)/shard_map/all_to_all | solution.py:244
  46.0 0.0 copy-done
  46.0 9.5 %collective-permute-start.5 = (bf16[448,256]{1,0:T(8,128)(2,1)S(1)}, bf16[448,256]{1,0:T(8,128)(2,1)S(1)}, u32[]{:S(2)}, u32[]{:S(2)}) collective-permute-start(bf16[448,256]{1,0:T(8,128)(2,1)S(1)} %copy-done), channel_id=1, source_target_pairs={{0,384},{48,432},{96,480},{144,528},{192,576},{240,624},{288,672},... | collective-permute-start | bytes 688136 | tf_op jit(solution)/shard_map/ppermute | solution.py:269
  55.5 16.2 %collective-permute-done.5.got_ref = bf16[448,256]{1,0:T(8,128)(2,1)S(1)} collective-permute-done((bf16[448,256]{1,0:T(8,128)(2,1)S(1)}, bf16[448,256]{1,0:T(8,128)(2,1)S(1)}, u32[]{:S(2)}, u32[]{:S(2)}) %collective-permute-start.5) | collective-permute-done | bytes 229408 | tf_op jit(solution)/shard_map/ppermute | solution.py:269
  71.7 2.3 %shard_map.68 = bf16[8,224,128]{2,1,0:T(8,128)(2,1)} custom-call(s32[1]{0:T(128)} %bitcast.half_ref, f32[448,1024]{1,0:T(8,128)} %bitcast.16, bf16[448,256]{1,0:T(8,128)(2,1)S(1)} %collective-permute-done.5.got_ref), custom_call_target="tpu_custom_call" | custom-call | tf_op jit(solution)/shard_map/pallas_call | solution.py:230
  74.1 0.0 all-to-all-done.2.in_ref
  74.1 4.8 %all-to-all-start.1 = ((bf16[8,224,128]{2,1,0:T(8,128)(2,1)}), bf16[8,224,128]{2,1,0:T(8,128)(2,1)S(1)}, u32[]{:S(2)}, u32[]{:S(2)}) async-start(bf16[8,224,128]{2,1,0:T(8,128)(2,1)} %shard_map.68), calls=%async_computation.1 | async-start | bytes 917504 | tf_op jit(solution)/shard_map/all_to_all | solution.py:244
  78.9 1.1 turnq.1
  80.0 9.5 %collective-permute-start.6 = (bf16[32,3584]{1,0:T(8,128)(2,1)}, bf16[32,3584]{1,0:T(8,128)(2,1)S(1)}, u32[]{:S(2)}, u32[]{:S(2)}) collective-permute-start(bf16[32,3584]{1,0:T(8,128)(2,1)} %get-tuple-element.29), channel_id=1, source_target_pairs={{0,384},{48,432},{96,480},{144,528},{192,576},{240,624},{288,672},... | collective-permute-start | bytes 688136 | tf_op jit(solution)/shard_map/ppermute | solution.py:290
  89.5 0.0 collective-permute-done.b_ref
  89.5 1.1 addcores.1
  90.6 3.4 %collective-permute-start.1 = (f32[288,128]{1,0:T(8,128)S(1)}, f32[288,128]{1,0:T(8,128)S(1)}, u32[]{:S(2)}, u32[]{:S(2)}) collective-permute-start(f32[288,128]{1,0:T(8,128)S(1)} %get-tuple-element.22), channel_id=1, source_target_pairs={{0,96},{48,144},{96,192},{144,240},{192,288},{240,336},{288,0},{33... | collective-permute-start | bytes 442376 | tf_op jit(solution)/shard_map/ppermute | solution.py:317
  94.0 2.5 %collective-permute-start.2 = (f32[288,128]{1,0:T(8,128)S(1)}, f32[288,128]{1,0:T(8,128)S(1)}, u32[]{:S(2)}, u32[]{:S(2)}) collective-permute-start(f32[288,128]{1,0:T(8,128)S(1)} %get-tuple-element.23), channel_id=1, source_target_pairs={{0,192},{48,240},{96,288},{144,336},{192,0},{240,48},{288,96},{336... | collective-permute-start | bytes 442376 | tf_op jit(solution)/shard_map/ppermute | solution.py:317
  96.5 4.5 %collective-permute-start.3 = (f32[288,128]{1,0:T(8,128)S(1)}, f32[288,128]{1,0:T(8,128)S(1)}, u32[]{:S(2)}, u32[]{:S(2)}) collective-permute-start(f32[288,128]{1,0:T(8,128)S(1)} %get-tuple-element.24), channel_id=1, source_target_pairs={{0,288},{48,336},{96,0},{144,48},{192,96},{240,144},{288,192},{336... | collective-permute-start | bytes 442376 | tf_op jit(solution)/shard_map/ppermute | solution.py:317
  101.1 0.0 collective-permute-done.1.b_ref
  101.1 2.9 %collective-permute-done.2.c_ref = f32[288,128]{1,0:T(8,128)S(1)} collective-permute-done((f32[288,128]{1,0:T(8,128)S(1)}, f32[288,128]{1,0:T(8,128)S(1)}, u32[]{:S(2)}, u32[]{:S(2)}) %collective-permute-start.2) | collective-permute-done | bytes 147488 | tf_op jit(solution)/shard_map/ppermute | solution.py:317
  103.9 1.9 %collective-permute-done.3.d_ref = f32[288,128]{1,0:T(8,128)S(1)} collective-permute-done((f32[288,128]{1,0:T(8,128)S(1)}, f32[288,128]{1,0:T(8,128)S(1)}, u32[]{:S(2)}, u32[]{:S(2)}) %collective-permute-start.3) | collective-permute-done | bytes 147488 | tf_op jit(solution)/shard_map/ppermute | solution.py:317
  105.9 2.7 %collective-permute-start.4 = (f32[144,128]{1,0:T(8,128)S(1)}, f32[144,128]{1,0:T(8,128)S(1)}, u32[]{:S(2)}, u32[]{:S(2)}) collective-permute-start(f32[144,128]{1,0:T(8,128)S(1)} %get-tuple-element.26), channel_id=1, source_target_pairs={{0,384},{48,432},{96,480},{144,528},{192,576},{240,624},{288,672},... | collective-permute-start | bytes 221192 | tf_op jit(solution)/shard_map/ppermute | solution.py:329
  108.6 0.0 all-to-all-done.1.p_ref
  108.6 0.0 collective-permute-done.6.got_ref
  108.6 1.4 %join.1 = bf16[64,7168]{1,0:T(8,128)(2,1)} custom-call(s32[1]{0:T(128)} %bitcast.half_ref, bf16[8,224,128]{2,1,0:T(8,128)(2,1)S(1)} %all-to-all-done.1.p_ref, bf16[32,3584]{1,0:T(8,128)(2,1)S(1)} %get-tuple-element.28.keep_ref, bf16[32,3584]{1,0:T(8,128)(2,1)S(1)} %collective-permute-done.6.got_ref), custom_call_target="tpu_custom_call" | custom-call | tf_op jit(solution)/shard_map/join/pallas_call | solution.py:338
  110.0 8.4 %collective-permute-done.4.b_ref = f32[144,128]{1,0:T(8,128)S(1)} collective-permute-done((f32[144,128]{1,0:T(8,128)S(1)}, f32[144,128]{1,0:T(8,128)S(1)}, u32[]{:S(2)}, u32[]{:S(2)}) %collective-permute-start.4) | collective-permute-done | bytes 73760 | tf_op jit(solution)/shard_map/ppermute | solution.py:329
  118.5 0.6 hidden.1
  (1 shorter events, 0.0 us)
Async XLA Ops:
  3.5 31.2 %all-to-all-start = ((bf16[48,16,128]{2,1,0:T(8,128)(2,1)}), bf16[48,16,128]{2,1,0:T(8,128)(2,1)S(1)}, u32[]{:S(2)}, u32[]{:S(2)}) async-start(bf16[48,16,128]{2,1,0:T(8,128)(2,1)} %bitcast.20), calls=%async_computation | async-start | bytes 393216 | tf_op jit(solution)/shard_map/all_to_all | solution.py:270
  36.3 9.7 %copy-start = (bf16[448,256]{1,0:T(8,128)(2,1)S(1)}, bf16[448,256]{1,0:T(8,128)(2,1)}, u32[]{:S(2)}) copy-start(bf16[448,256]{1,0:T(8,128)(2,1)} %get-tuple-element.27) | copy-start | bytes 688132
  36.3 53.2 %collective-permute-start = (f32[4,288,128]{2,1,0:T(8,128)S(1)}, f32[4,288,128]{2,1,0:T(8,128)S(1)}, u32[]{:S(2)}, u32[]{:S(2)}) collective-permute-start(f32[4,288,128]{2,1,0:T(8,128)S(1)} %get-tuple-element.20), channel_id=1, source_target_pairs={{0,48},{48,0},{96,144},{144,96},{192,240},{240,192},{288,336},{336... | collective-permute-start | bytes 1769480 | tf_op jit(solution)/shard_map/ppermute | solution.py:307
  41.0 33.0 %all-to-all-start.2 = ((bf16[8,224,128]{2,1,0:T(8,128)(2,1)}), bf16[8,224,128]{2,1,0:T(8,128)(2,1)S(1)}, u32[]{:S(2)}, u32[]{:S(2)}) async-start(bf16[8,224,128]{2,1,0:T(8,128)(2,1)} %splitq.1), calls=%async_computation.2 | async-start | bytes 917504 | tf_op jit(solution)/shard_map/all_to_all | solution.py:244
  46.0 25.7 %collective-permute-start.5 = (bf16[448,256]{1,0:T(8,128)(2,1)S(1)}, bf16[448,256]{1,0:T(8,128)(2,1)S(1)}, u32[]{:S(2)}, u32[]{:S(2)}) collective-permute-start(bf16[448,256]{1,0:T(8,128)(2,1)S(1)} %copy-done), channel_id=1, source_target_pairs={{0,384},{48,432},{96,480},{144,528},{192,576},{240,624},{288,672},... | collective-permute-start | bytes 688136 | tf_op jit(solution)/shard_map/ppermute | solution.py:269
  74.1 34.5 %all-to-all-start.1 = ((bf16[8,224,128]{2,1,0:T(8,128)(2,1)}), bf16[8,224,128]{2,1,0:T(8,128)(2,1)S(1)}, u32[]{:S(2)}, u32[]{:S(2)}) async-start(bf16[8,224,128]{2,1,0:T(8,128)(2,1)} %shard_map.68), calls=%async_computation.1 | async-start | bytes 917504 | tf_op jit(solution)/shard_map/all_to_all | solution.py:244
  80.0 28.6 %collective-permute-start.6 = (bf16[32,3584]{1,0:T(8,128)(2,1)}, bf16[32,3584]{1,0:T(8,128)(2,1)S(1)}, u32[]{:S(2)}, u32[]{:S(2)}) collective-permute-start(bf16[32,3584]{1,0:T(8,128)(2,1)} %get-tuple-element.29), channel_id=1, source_target_pairs={{0,384},{48,432},{96,480},{144,528},{192,576},{240,624},{288,672},... | collective-permute-start | bytes 688136 | tf_op jit(solution)/shard_map/ppermute | solution.py:290
  90.6 10.5 %collective-permute-start.1 = (f32[288,128]{1,0:T(8,128)S(1)}, f32[288,128]{1,0:T(8,128)S(1)}, u32[]{:S(2)}, u32[]{:S(2)}) collective-permute-start(f32[288,128]{1,0:T(8,128)S(1)} %get-tuple-element.22), channel_id=1, source_target_pairs={{0,96},{48,144},{96,192},{144,240},{192,288},{240,336},{288,0},{33... | collective-permute-start | bytes 442376 | tf_op jit(solution)/shard_map/ppermute | solution.py:317
  94.0 9.9 %collective-permute-start.2 = (f32[288,128]{1,0:T(8,128)S(1)}, f32[288,128]{1,0:T(8,128)S(1)}, u32[]{:S(2)}, u32[]{:S(2)}) collective-permute-start(f32[288,128]{1,0:T(8,128)S(1)} %get-tuple-element.23), channel_id=1, source_target_pairs={{0,192},{48,240},{96,288},{144,336},{192,0},{240,48},{288,96},{336... | collective-permute-start | bytes 442376 | tf_op jit(solution)/shard_map/ppermute | solution.py:317
  96.5 9.3 %collective-permute-start.3 = (f32[288,128]{1,0:T(8,128)S(1)}, f32[288,128]{1,0:T(8,128)S(1)}, u32[]{:S(2)}, u32[]{:S(2)}) collective-permute-start(f32[288,128]{1,0:T(8,128)S(1)} %get-tuple-element.24), channel_id=1, source_target_pairs={{0,288},{48,336},{96,0},{144,48},{192,96},{240,144},{288,192},{336... | collective-permute-start | bytes 442376 | tf_op jit(solution)/shard_map/ppermute | solution.py:317
  105.9 12.6 %collective-permute-start.4 = (f32[144,128]{1,0:T(8,128)S(1)}, f32[144,128]{1,0:T(8,128)S(1)}, u32[]{:S(2)}, u32[]{:S(2)}) collective-permute-start(f32[144,128]{1,0:T(8,128)S(1)} %get-tuple-element.26), channel_id=1, source_target_pairs={{0,384},{48,432},{96,480},{144,528},{192,576},{240,624},{288,672},... | collective-permute-start | bytes 221192 | tf_op jit(solution)/shard_map/ppermute | solution.py:329

commit v3 on v2

--- a/solution.py
+++ b/solution.py
@@ -31,7 +31,7 @@
     return pl.BlockSpec(memory_space=pltpu.SMEM)
 
 
-def packed(ids_ref, tokens_ref):
+def pack_kernel(ids_ref, tokens_ref, out_ref):
     n = EXPERTS * 16
     rows = tokens_ref.shape[0]
     width = tokens_ref.shape[1]
@@ -53,7 +53,7 @@
             part = jnp.concatenate([part, jnp.zeros((rows, LANES - part.shape[1]), BF16)], axis=1)
         pick = jnp.where((line & 3) == b, taken, 0.0).astype(BF16)
         total = total + jnp.dot(pick, part, preferred_element_type=F32)
-    return total.astype(BF16)
+    out_ref[...] = total.astype(BF16)
 
 
 def project_kernel(core_ref, got_ref, gate_ref, up_ref, keep_ref, send_ref):
@@ -133,24 +133,13 @@
     return out.astype(BF16)
 
 
-def prepare_kernel(half_ref, ids_ref, tokens_ref, down_ref, rows_ref, p_ref, down, rows, p, sems):
-    lanes = pl.ds(pl.multiple_of((1 - half_ref[0]) * 512, LANES), 512)
-    load = pltpu.make_async_copy(down_ref.at[:, lanes], down, sems.at[0])
-    store_rows = pltpu.make_async_copy(rows, rows_ref, sems.at[1])
-    store_p = pltpu.make_async_copy(p, p_ref, sems.at[2])
-    load.start()
-    rows[...] = packed(ids_ref, tokens_ref)
-    store_rows.start()
-    load.wait()
+def narrow_kernel(half_ref, down_ref, out_ref):
     for t in range(2):
         parts = []
         for j in range(4 * t, 4 * t + 4):
             k = j // 2 * LANES
-            parts.append((down[:, k : k + LANES], j % 2 * 64))
-        p[:, t * LANES : (t + 1) * LANES] = quarters(parts)
-    store_p.start()
-    store_rows.wait()
-    store_p.wait()
+            parts.append((down_ref[:, k : k + LANES], j % 2 * 64))
+        out_ref[:, t * LANES : (t + 1) * LANES] = quarters(parts)
 
 
 def split_p_kernel(half_ref, down_ref, got_ref, out_ref):
@@ -254,21 +243,18 @@
     place = ((owner >> 1) & 3).astype(jnp.int32).reshape(1)
     down = jnp.swapaxes(trainer_down, 1, 2).reshape(width, 1024)
 
-    shapes = [(EXPERTS * 16, LANES), (width, 256)]
-    anywhere = pl.BlockSpec(memory_space=pl.ANY)
-    slots, outgoing = pl.pallas_call(
-        prepare_kernel,
-        out_shape=[jax.ShapeDtypeStruct(shape, BF16) for shape in shapes],
-        in_specs=[smem()] + [vmem()] * 2 + [anywhere],
-        out_specs=[anywhere] * 2,
-        scratch_shapes=[pltpu.VMEM((width, 512), F32)]
-        + [pltpu.VMEM(shape, BF16) for shape in shapes]
-        + [pltpu.SemaphoreType.DMA((3,))],
-        name="prepare",
-    )(half, expert_ids.T, tokens, down)
+    outgoing = half_of_down(narrow_kernel, (width, 256), half, down, True)
     incoming = lax.ppermute(outgoing, "owner", SWAP_HALF)
+
+    packed = pl.pallas_call(
+        pack_kernel,
+        out_shape=jax.ShapeDtypeStruct((EXPERTS * 16, LANES), BF16),
+        in_specs=[vmem(), vmem()],
+        out_specs=vmem(),
+        name="pack",
+    )(expert_ids.T, tokens)
     got = lax.all_to_all(
-        slots.reshape(EXPERTS, 16, LANES), "shard", split_axis=0, concat_axis=0, tiled=True
+        packed.reshape(EXPERTS, 16, LANES), "shard", split_axis=0, concat_axis=0, tiled=True
     )
 
     pieces = (8, width // 2, LANES)

time: 120 us -> 121 us (level)
  Pallas kernels: 15.4 us -> 16.9 us
    pallas_call x1 -> x2, Pallas kernels: 2.35 us -> 4.49 us  [half_of_down(): pl.pallas_call(kernel, out_shape=jax.ShapeDtypeStruct(out, BF16), grid_sp...]
  transfers between devices with their start and end apart: 10 -> 10, of which waited for: 5 -> 5; matrix products, arithmetic and copies ran while one was open for 0% -> 0% of each run, Pallas kernels for 9% -> 10%
where the time goes in v3:
time: 121 us
  starting transfers between devices  61.1 us (50%)
  waiting for transfers between devices  41.9 us (35%)
  Pallas kernels  16.9 us (14%)
    all_to_all x1, starting transfers between devices, on_device(): lax.all_to_all(packed.reshape(EXPERTS, 16, LANES), 'shard', split_axis=0,...  17.4 us
    ppermute x1, waiting for transfers between devices, on_device(): incoming = lax.ppermute(outgoing, 'owner', SWAP_HALF)  16.4 us
    all_to_all x1, waiting for transfers between devices, on_device(): lax.all_to_all(packed.reshape(EXPERTS, 16, LANES), 'shard', split_axis=0,...  12.3 us
    ppermute x3, starting transfers between devices, on_device(): summed.append(lax.ppermute(sums[d], 'owner', ALONG_X[d]))  10.4 us
    all_to_all x2, starting transfers between devices, over_x(): lax.all_to_all(x, 'owner', split_axis=0, concat_axis=0, tiled=True, axis_...  9.74 us
    ppermute x1, starting transfers between devices, on_device(): incoming = lax.ppermute(outgoing, 'owner', SWAP_HALF)  9.51 us
    ppermute x1, starting transfers between devices, on_device(): q_got = lax.ppermute(q_send, 'owner', SWAP_HALF)  9.48 us
    ppermute x1, waiting for transfers between devices, on_device(): added = lax.ppermute(theirs, 'owner', SWAP_HALF)  8.42 us
  transfers between devices with their start and end apart: 10, of which 5 were waited for; matrix products, arithmetic and copies ran while one was open for 0% of the time, Pallas kernels for 10%

profile of v3, /device:TPU:66, one launch (start us, length us, event | category | flops | bytes accessed | tf_op | source)
XLA Modules:
  0.0 120.7 jit_solution(4822964120707881032)
XLA Ops:
  0.6 2.3 %pack.1 = bf16[768,128]{1,0:T(8,128)(2,1)} custom-call(s32[8,12]{1,0:T(8,128)} %bitcast.22, bf16[12,448]{1,0:T(8,128)(2,1)} %tokens_ref.1), custom_call_target="tpu_custom_call" | custom-call | tf_op jit(solution)/shard_map/pack/pallas_call | solution.py:249
  2.9 17.4 %all-to-all-start = ((bf16[48,16,128]{2,1,0:T(8,128)(2,1)}), bf16[48,16,128]{2,1,0:T(8,128)(2,1)S(1)}, u32[]{:S(2)}, u32[]{:S(2)}) async-start(bf16[48,16,128]{2,1,0:T(8,128)(2,1)} %bitcast.20), calls=%async_computation | async-start | bytes 393216 | tf_op jit(solution)/shard_map/all_to_all | solution.py:256
  20.3 1.5 %load.1 = (bf16[448,1024]{1,0:T(8,128)(2,1)S(1)}, bf16[448,1024]{1,0:T(8,128)(2,1)S(1)}) custom-call(bf16[448,1024]{1,0:T(8,128)(2,1)} %bitcast.17, bf16[448,1024]{1,0:T(8,128)(2,1)} %bitcast.18), custom_call_target="tpu_custom_call" | custom-call | tf_op jit(solution)/shard_map/load/pallas_call | solution.py:278
  21.8 12.3 %all-to-all-done = bf16[48,16,128]{2,1,0:T(8,128)(2,1)S(1)} async-done(((bf16[48,16,128]{2,1,0:T(8,128)(2,1)}), bf16[48,16,128]{2,1,0:T(8,128)(2,1)S(1)}, u32[]{:S(2)}, u32[]{:S(2)}) %all-to-all-start) | async-done | bytes 196640 | tf_op jit(solution)/shard_map/all_to_all | solution.py:256
  34.0 1.6 %project.1 = (f32[4,288,128]{2,1,0:T(8,128)}, f32[4,288,128]{2,1,0:T(8,128)S(1)}) custom-call(s32[1]{0:T(128)} %bitcast.2.core_ref, bf16[768,128]{1,0:T(8,128)(2,1)S(1)} %bitcast.13, bf16[448,1024]{1,0:T(8,128)(2,1)S(1)} %get-tuple-element.14.gate_ref, bf16[448,1024]{1,0:T(8,128)(2,1)S(1)} %get-tuple-element.15.up_ref), custom_call_target="tpu_custom_call" | custom-call | tf_op jit(solution)/shard_map/project/pallas_call | solution.py:286
  35.7 1.9 %collective-permute-start = (f32[4,288,128]{2,1,0:T(8,128)S(1)}, f32[4,288,128]{2,1,0:T(8,128)S(1)}, u32[]{:S(2)}, u32[]{:S(2)}) collective-permute-start(f32[4,288,128]{2,1,0:T(8,128)S(1)} %get-tuple-element.17), channel_id=1, source_target_pairs={{0,48},{48,0},{96,144},{144,96},{192,240},{240,192},{288,336},{336... | collective-permute-start | bytes 1769480 | tf_op jit(solution)/shard_map/ppermute | solution.py:293
  37.6 2.7 %splitq.1 = bf16[8,224,128]{2,1,0:T(8,128)(2,1)} custom-call(f32[448,1024]{1,0:T(8,128)} %bitcast.14), custom_call_target="tpu_custom_call" | custom-call | tf_op jit(solution)/shard_map/splitq/pallas_call | solution.py:261
  40.3 4.9 %all-to-all-start.2 = ((bf16[8,224,128]{2,1,0:T(8,128)(2,1)}), bf16[8,224,128]{2,1,0:T(8,128)(2,1)S(1)}, u32[]{:S(2)}, u32[]{:S(2)}) async-start(bf16[8,224,128]{2,1,0:T(8,128)(2,1)} %splitq.1), calls=%async_computation.2 | async-start | bytes 917504 | tf_op jit(solution)/shard_map/all_to_all | solution.py:233
  45.2 2.1 %shard_map.68 = bf16[448,256]{1,0:T(8,128)(2,1)} custom-call(s32[1]{0:T(128)} %bitcast.half_ref, f32[448,1024]{1,0:T(8,128)} %bitcast.15), custom_call_target="tpu_custom_call" | custom-call | tf_op jit(solution)/shard_map/pallas_call | solution.py:219
  47.3 9.5 %collective-permute-start.5 = (bf16[448,256]{1,0:T(8,128)(2,1)}, bf16[448,256]{1,0:T(8,128)(2,1)S(1)}, u32[]{:S(2)}, u32[]{:S(2)}) collective-permute-start(bf16[448,256]{1,0:T(8,128)(2,1)} %shard_map.68), channel_id=1, source_target_pairs={{0,384},{48,432},{96,480},{144,528},{192,576},{240,624},{288,672},... | collective-permute-start | bytes 688136 | tf_op jit(solution)/shard_map/ppermute | solution.py:247
  56.9 16.4 %collective-permute-done.5.got_ref = bf16[448,256]{1,0:T(8,128)(2,1)S(1)} collective-permute-done((bf16[448,256]{1,0:T(8,128)(2,1)}, bf16[448,256]{1,0:T(8,128)(2,1)S(1)}, u32[]{:S(2)}, u32[]{:S(2)}) %collective-permute-start.5) | collective-permute-done | bytes 229408 | tf_op jit(solution)/shard_map/ppermute | solution.py:247
  73.3 2.4 %shard_map.69 = bf16[8,224,128]{2,1,0:T(8,128)(2,1)} custom-call(s32[1]{0:T(128)} %bitcast.half_ref, f32[448,1024]{1,0:T(8,128)} %bitcast.16, bf16[448,256]{1,0:T(8,128)(2,1)S(1)} %collective-permute-done.5.got_ref), custom_call_target="tpu_custom_call" | custom-call | tf_op jit(solution)/shard_map/pallas_call | solution.py:219
  75.6 0.0 all-to-all-done.2.in_ref
  75.6 4.8 %all-to-all-start.1 = ((bf16[8,224,128]{2,1,0:T(8,128)(2,1)}), bf16[8,224,128]{2,1,0:T(8,128)(2,1)S(1)}, u32[]{:S(2)}, u32[]{:S(2)}) async-start(bf16[8,224,128]{2,1,0:T(8,128)(2,1)} %shard_map.69), calls=%async_computation.1 | async-start | bytes 917504 | tf_op jit(solution)/shard_map/all_to_all | solution.py:233
  80.4 1.1 turnq.1
  81.6 9.5 %collective-permute-start.6 = (bf16[32,3584]{1,0:T(8,128)(2,1)}, bf16[32,3584]{1,0:T(8,128)(2,1)S(1)}, u32[]{:S(2)}, u32[]{:S(2)}) collective-permute-start(bf16[32,3584]{1,0:T(8,128)(2,1)} %get-tuple-element.25), channel_id=1, source_target_pairs={{0,384},{48,432},{96,480},{144,528},{192,576},{240,624},{288,672},... | collective-permute-start | bytes 688136 | tf_op jit(solution)/shard_map/ppermute | solution.py:276
  91.1 0.0 collective-permute-done.b_ref
  91.1 1.1 addcores.1
  92.2 3.4 %collective-permute-start.1 = (f32[288,128]{1,0:T(8,128)S(1)}, f32[288,128]{1,0:T(8,128)S(1)}, u32[]{:S(2)}, u32[]{:S(2)}) collective-permute-start(f32[288,128]{1,0:T(8,128)S(1)} %get-tuple-element.19), channel_id=1, source_target_pairs={{0,96},{48,144},{96,192},{144,240},{192,288},{240,336},{288,0},{33... | collective-permute-start | bytes 442376 | tf_op jit(solution)/shard_map/ppermute | solution.py:303
  95.6 2.5 %collective-permute-start.2 = (f32[288,128]{1,0:T(8,128)S(1)}, f32[288,128]{1,0:T(8,128)S(1)}, u32[]{:S(2)}, u32[]{:S(2)}) collective-permute-start(f32[288,128]{1,0:T(8,128)S(1)} %get-tuple-element.20), channel_id=1, source_target_pairs={{0,192},{48,240},{96,288},{144,336},{192,0},{240,48},{288,96},{336... | collective-permute-start | bytes 442376 | tf_op jit(solution)/shard_map/ppermute | solution.py:303
  98.1 4.5 %collective-permute-start.3 = (f32[288,128]{1,0:T(8,128)S(1)}, f32[288,128]{1,0:T(8,128)S(1)}, u32[]{:S(2)}, u32[]{:S(2)}) collective-permute-start(f32[288,128]{1,0:T(8,128)S(1)} %get-tuple-element.21), channel_id=1, source_target_pairs={{0,288},{48,336},{96,0},{144,48},{192,96},{240,144},{288,192},{336... | collective-permute-start | bytes 442376 | tf_op jit(solution)/shard_map/ppermute | solution.py:303
  102.6 0.0 collective-permute-done.1.b_ref
  102.7 2.9 %collective-permute-done.2.c_ref = f32[288,128]{1,0:T(8,128)S(1)} collective-permute-done((f32[288,128]{1,0:T(8,128)S(1)}, f32[288,128]{1,0:T(8,128)S(1)}, u32[]{:S(2)}, u32[]{:S(2)}) %collective-permute-start.2) | collective-permute-done | bytes 147488 | tf_op jit(solution)/shard_map/ppermute | solution.py:303
  105.5 1.9 %collective-permute-done.3.d_ref = f32[288,128]{1,0:T(8,128)S(1)} collective-permute-done((f32[288,128]{1,0:T(8,128)S(1)}, f32[288,128]{1,0:T(8,128)S(1)}, u32[]{:S(2)}, u32[]{:S(2)}) %collective-permute-start.3) | collective-permute-done | bytes 147488 | tf_op jit(solution)/shard_map/ppermute | solution.py:303
  107.5 2.7 %collective-permute-start.4 = (f32[144,128]{1,0:T(8,128)S(1)}, f32[144,128]{1,0:T(8,128)S(1)}, u32[]{:S(2)}, u32[]{:S(2)}) collective-permute-start(f32[144,128]{1,0:T(8,128)S(1)} %get-tuple-element.23), channel_id=1, source_target_pairs={{0,384},{48,432},{96,480},{144,528},{192,576},{240,624},{288,672},... | collective-permute-start | bytes 221192 | tf_op jit(solution)/shard_map/ppermute | solution.py:315
  110.2 0.0 all-to-all-done.1.p_ref
  110.2 0.0 collective-permute-done.6.got_ref
  110.2 1.4 %join.1 = bf16[64,7168]{1,0:T(8,128)(2,1)} custom-call(s32[1]{0:T(128)} %bitcast.half_ref, bf16[8,224,128]{2,1,0:T(8,128)(2,1)S(1)} %all-to-all-done.1.p_ref, bf16[32,3584]{1,0:T(8,128)(2,1)S(1)} %get-tuple-element.24.keep_ref, bf16[32,3584]{1,0:T(8,128)(2,1)S(1)} %collective-permute-done.6.got_ref), custom_call_target="tpu_custom_call" | custom-call | tf_op jit(solution)/shard_map/join/pallas_call | solution.py:324
  111.6 8.4 %collective-permute-done.4.b_ref = f32[144,128]{1,0:T(8,128)S(1)} collective-permute-done((f32[144,128]{1,0:T(8,128)S(1)}, f32[144,128]{1,0:T(8,128)S(1)}, u32[]{:S(2)}, u32[]{:S(2)}) %collective-permute-start.4) | collective-permute-done | bytes 73760 | tf_op jit(solution)/shard_map/ppermute | solution.py:315
  120.0 0.6 hidden.1
  (1 shorter events, 0.0 us)
Async XLA Ops:
  2.9 31.1 %all-to-all-start = ((bf16[48,16,128]{2,1,0:T(8,128)(2,1)}), bf16[48,16,128]{2,1,0:T(8,128)(2,1)S(1)}, u32[]{:S(2)}, u32[]{:S(2)}) async-start(bf16[48,16,128]{2,1,0:T(8,128)(2,1)} %bitcast.20), calls=%async_computation | async-start | bytes 393216 | tf_op jit(solution)/shard_map/all_to_all | solution.py:256
  35.7 55.4 %collective-permute-start = (f32[4,288,128]{2,1,0:T(8,128)S(1)}, f32[4,288,128]{2,1,0:T(8,128)S(1)}, u32[]{:S(2)}, u32[]{:S(2)}) collective-permute-start(f32[4,288,128]{2,1,0:T(8,128)S(1)} %get-tuple-element.17), channel_id=1, source_target_pairs={{0,48},{48,0},{96,144},{144,96},{192,240},{240,192},{288,336},{336... | collective-permute-start | bytes 1769480 | tf_op jit(solution)/shard_map/ppermute | solution.py:293
  40.3 35.4 %all-to-all-start.2 = ((bf16[8,224,128]{2,1,0:T(8,128)(2,1)}), bf16[8,224,128]{2,1,0:T(8,128)(2,1)S(1)}, u32[]{:S(2)}, u32[]{:S(2)}) async-start(bf16[8,224,128]{2,1,0:T(8,128)(2,1)} %splitq.1), calls=%async_computation.2 | async-start | bytes 917504 | tf_op jit(solution)/shard_map/all_to_all | solution.py:233
  47.3 25.9 %collective-permute-start.5 = (bf16[448,256]{1,0:T(8,128)(2,1)}, bf16[448,256]{1,0:T(8,128)(2,1)S(1)}, u32[]{:S(2)}, u32[]{:S(2)}) collective-permute-start(bf16[448,256]{1,0:T(8,128)(2,1)} %shard_map.68), channel_id=1, source_target_pairs={{0,384},{48,432},{96,480},{144,528},{192,576},{240,624},{288,672},... | collective-permute-start | bytes 688136 | tf_op jit(solution)/shard_map/ppermute | solution.py:247
  75.6 34.5 %all-to-all-start.1 = ((bf16[8,224,128]{2,1,0:T(8,128)(2,1)}), bf16[8,224,128]{2,1,0:T(8,128)(2,1)S(1)}, u32[]{:S(2)}, u32[]{:S(2)}) async-start(bf16[8,224,128]{2,1,0:T(8,128)(2,1)} %shard_map.69), calls=%async_computation.1 | async-start | bytes 917504 | tf_op jit(solution)/shard_map/all_to_all | solution.py:233
  81.6 28.6 %collective-permute-start.6 = (bf16[32,3584]{1,0:T(8,128)(2,1)}, bf16[32,3584]{1,0:T(8,128)(2,1)S(1)}, u32[]{:S(2)}, u32[]{:S(2)}) collective-permute-start(bf16[32,3584]{1,0:T(8,128)(2,1)} %get-tuple-element.25), channel_id=1, source_target_pairs={{0,384},{48,432},{96,480},{144,528},{192,576},{240,624},{288,672},... | collective-permute-start | bytes 688136 | tf_op jit(solution)/shard_map/ppermute | solution.py:276
  92.2 10.5 %collective-permute-start.1 = (f32[288,128]{1,0:T(8,128)S(1)}, f32[288,128]{1,0:T(8,128)S(1)}, u32[]{:S(2)}, u32[]{:S(2)}) collective-permute-start(f32[288,128]{1,0:T(8,128)S(1)} %get-tuple-element.19), channel_id=1, source_target_pairs={{0,96},{48,144},{96,192},{144,240},{192,288},{240,336},{288,0},{33... | collective-permute-start | bytes 442376 | tf_op jit(solution)/shard_map/ppermute | solution.py:303
  95.6 9.9 %collective-permute-start.2 = (f32[288,128]{1,0:T(8,128)S(1)}, f32[288,128]{1,0:T(8,128)S(1)}, u32[]{:S(2)}, u32[]{:S(2)}) collective-permute-start(f32[288,128]{1,0:T(8,128)S(1)} %get-tuple-element.20), channel_id=1, source_target_pairs={{0,192},{48,240},{96,288},{144,336},{192,0},{240,48},{288,96},{336... | collective-permute-start | bytes 442376 | tf_op jit(solution)/shard_map/ppermute | solution.py:303
  98.1 9.3 %collective-permute-start.3 = (f32[288,128]{1,0:T(8,128)S(1)}, f32[288,128]{1,0:T(8,128)S(1)}, u32[]{:S(2)}, u32[]{:S(2)}) collective-permute-start(f32[288,128]{1,0:T(8,128)S(1)} %get-tuple-element.21), channel_id=1, source_target_pairs={{0,288},{48,336},{96,0},{144,48},{192,96},{240,144},{288,192},{336... | collective-permute-start | bytes 442376 | tf_op jit(solution)/shard_map/ppermute | solution.py:303
  107.5 12.6 %collective-permute-start.4 = (f32[144,128]{1,0:T(8,128)S(1)}, f32[144,128]{1,0:T(8,128)S(1)}, u32[]{:S(2)}, u32[]{:S(2)}) collective-permute-start(f32[144,128]{1,0:T(8,128)S(1)} %get-tuple-element.23), channel_id=1, source_target_pairs={{0,384},{48,432},{96,480},{144,528},{192,576},{240,624},{288,672},... | collective-permute-start | bytes 221192 | tf_op jit(solution)/shard_map/ppermute | solution.py:315
